TPU v7x, 32 devices: a whole 2x2x4 slice. The times are simulated.
32 devices in a mesh: ctx: 4 (over y, x), head: 8 (over z, core).
Axes of the slice: x: 2, y: 2, z: 4, core: 2. Of those that a mesh axis runs over, the one named last changes fastest.
Arguments:
- state: bfloat16 [4096, 2048], P('ctx'), may hold values from -6 to 6
- norm_gain: bfloat16 [2048], replicated, may hold values from 0.5 to 1.5
- w_qkv: bfloat16 [3, 2048, 2048], P(None, None, 'head'), may hold values from -2 to 2
- w_out: bfloat16 [2048, 2048], P('head'), may hold values from -0.125 to 0.125
- probe: bfloat16 [4096, 2048], P('ctx'), may hold values from -6 to 6
- noise: bfloat16 [4096, 2048], P(('ctx', 'head')), may hold values from -6 to 6
- segment_ids: int32 [4096], P('ctx'), may hold values from 0 to 2, never falling along the last dimension, each value on 1 to 3072 neighbouring positions
Outputs:
- new_state: float32 [4096, 2048], P(('ctx', 'head'))
Inputs may be any that keep to these rules, and one draw needn't show every extreme that they name: `segment_ids`: segment numbers never fall along the sequence; a segment holds at most 3072 positions.
All inputs are finite; a program needn't handle non-finite values.
Results may differ from a plain program's by a relative error of at most 0.011.
Values may be sent and summed in bfloat16 or wider, within the bound.
A program may use at most 128 MiB of HBM per device.

v0:
```python
import jax
import jax.numpy as jnp
from jax import lax
from jax.sharding import PartitionSpec as P

HEAD_DIM = 128


EPSILON = 1e-05
STEP_SIZE = 0.25
NEGATIVE = -1e30


def row_scale(matrix):
    return lax.rsqrt(jnp.mean(matrix * matrix, axis=-1, keepdims=True) + EPSILON)


def readout_grad(layer_out, probe_full):
    scale_y = row_scale(layer_out)
    return scale_y * probe_full - layer_out * scale_y**3 * jnp.mean(
        probe_full * layer_out, axis=-1, keepdims=True
    )


def over_blocks(block_fn, state_carry, arrays, begin_row, block_limit):
    row_count = arrays[0].shape[0]
    block_size = min(row_count, block_limit)
    number = row_count // block_size
    stacked = tuple((member.reshape((number, block_size) + member.shape[1:]) for member in arrays))
    offsets = begin_row + block_size * jnp.arange(number, dtype=jnp.int32)

    def advance(running, scan_item):
        return (block_fn(running, scan_item[0], scan_item[1]), None)

    state_carry, _ = lax.scan(advance, state_carry, (stacked, offsets))
    return state_carry


def body(state, norm_gain, w_qkv, w_out, probe, noise, segment_ids):
    local_rows, model_width = state.shape
    local_heads = w_qkv.shape[2] // HEAD_DIM
    score_scale = HEAD_DIM ** (-0.5)
    head_count = lax.axis_size("head")
    ctx_index = lax.axis_index("ctx")
    own_rows = local_rows // head_count
    row_start = lax.axis_index("head") * own_rows
    state_f = state.astype(jnp.float32)
    gain_full = norm_gain.astype(jnp.float32)
    inverse = row_scale(state_f)
    normed = (state_f * inverse * gain_full).astype(jnp.bfloat16)
    projected = jnp.einsum("sd,cdn->csn", normed, w_qkv, preferred_element_type=jnp.float32).astype(
        jnp.bfloat16
    )
    query_rows, key_rows, value_rows = (projected[0], projected[1], projected[2])
    queries = query_rows.reshape(local_rows, local_heads, HEAD_DIM).transpose(1, 0, 2)
    query_pos = ctx_index * local_rows + jnp.arange(local_rows, dtype=jnp.int32)

    def visible(key_seg, key_start):
        key_pos = key_start + jnp.arange(key_seg.shape[0], dtype=jnp.int32)
        return (
            (key_pos[None, :] <= query_pos[:, None]) & (key_seg[None, :] == segment_ids[:, None])
        )[None]

    def forward_block(state_carry, key_piece, key_start):
        run_max, run_sum, run_acc = state_carry
        block_rows = key_piece[0].shape[0]
        key_heads = key_piece[0].reshape(block_rows, local_heads, HEAD_DIM)
        value_heads = key_piece[1].reshape(block_rows, local_heads, HEAD_DIM)
        allowed = visible(key_piece[2], key_start)
        scores = (
            jnp.einsum("hqe,khe->hqk", queries, key_heads, preferred_element_type=jnp.float32)
            * score_scale
        )
        scores = jnp.where(allowed, scores, NEGATIVE)
        new_max = jnp.maximum(run_max, jnp.max(scores, axis=-1))
        weights = jnp.where(allowed, jnp.exp(scores - new_max[..., None]), 0.0)
        factor = jnp.exp(run_max - new_max)
        run_sum = run_sum * factor + jnp.sum(weights, axis=-1)
        run_acc = run_acc * factor[..., None] + jnp.einsum(
            "hqk,khe->hqe",
            weights.astype(jnp.bfloat16),
            value_heads,
            preferred_element_type=jnp.float32,
        )
        return (new_max, run_sum, run_acc)

    initial = (
        jnp.full((local_heads, local_rows), NEGATIVE, jnp.float32),
        jnp.zeros((local_heads, local_rows), jnp.float32),
        jnp.zeros((local_heads, local_rows, HEAD_DIM), jnp.float32),
    )
    all_keys, all_values, all_segs = (
        lax.all_gather(key_rows, "ctx", axis=0, tiled=True),
        lax.all_gather(value_rows, "ctx", axis=0, tiled=True),
        lax.all_gather(segment_ids, "ctx", axis=0, tiled=True),
    )
    run_max, run_sum, run_acc = over_blocks(
        forward_block, initial, (all_keys, all_values, all_segs), 0, local_rows
    )
    outputs = (run_acc / run_sum[..., None]).astype(jnp.bfloat16)
    log_totals = run_max + jnp.log(run_sum)
    out_rows = outputs.transpose(1, 0, 2).reshape(local_rows, local_heads * HEAD_DIM)
    state_own = lax.dynamic_slice_in_dim(state_f, row_start, own_rows, 0)
    inverse_own = lax.dynamic_slice_in_dim(inverse, row_start, own_rows, 0)
    term = jnp.dot(out_rows, w_out, preferred_element_type=jnp.float32)
    layer_out = state_f + lax.psum(term.astype(jnp.bfloat16), "head").astype(jnp.float32)
    readout_full = readout_grad(layer_out, probe.astype(jnp.float32))
    readout_half = readout_full.astype(jnp.bfloat16)
    readout_own = lax.dynamic_slice_in_dim(readout_full, row_start, own_rows, 0)
    grads_out = jnp.einsum(
        "sd,hed->hse",
        readout_half,
        w_out.reshape(local_heads, HEAD_DIM, model_width),
        preferred_element_type=jnp.float32,
    ).astype(jnp.bfloat16)
    deltas = jnp.sum(grads_out.astype(jnp.float32) * outputs.astype(jnp.float32), axis=-1)

    def back_block(key_block, value_block, seg_block, key_start):
        block_rows = key_block.shape[0]
        key_heads = key_block.reshape(block_rows, local_heads, HEAD_DIM)
        value_heads = value_block.reshape(block_rows, local_heads, HEAD_DIM)
        allowed = visible(seg_block, key_start)
        scores = (
            jnp.einsum("hqe,khe->hqk", queries, key_heads, preferred_element_type=jnp.float32)
            * score_scale
        )
        probabilities = jnp.where(
            allowed, jnp.exp(jnp.where(allowed, scores, NEGATIVE) - log_totals[..., None]), 0.0
        )
        dprobs = jnp.einsum(
            "hqe,khe->hqk", grads_out, value_heads, preferred_element_type=jnp.float32
        )
        dscores = probabilities * (dprobs - deltas[..., None])
        prob_half = probabilities.astype(jnp.bfloat16)
        dscore_half = dscores.astype(jnp.bfloat16)
        value_part = jnp.einsum(
            "hqk,hqe->khe", prob_half, grads_out, preferred_element_type=jnp.float32
        )
        key_part = (
            jnp.einsum("hqk,hqe->khe", dscore_half, queries, preferred_element_type=jnp.float32)
            * score_scale
        )
        query_part = (
            jnp.einsum("hqk,khe->hqe", dscore_half, key_heads, preferred_element_type=jnp.float32)
            * score_scale
        )
        return (query_part, key_part.reshape(block_rows, -1), value_part.reshape(block_rows, -1))

    query_zero = jnp.zeros((local_heads, local_rows, HEAD_DIM), jnp.float32)

    def add_query(running, key_piece, key_start):
        query_part, _, _ = back_block(key_piece[0], key_piece[1], key_piece[2], key_start)
        return running + query_part

    query_acc = over_blocks(add_query, query_zero, (all_keys, all_values, all_segs), 0, local_rows)
    row_count = local_rows * lax.axis_size("ctx")
    block_size = min(row_count, local_rows)
    number = row_count // block_size

    def one_block(block_index):
        offset = block_index * block_size
        key_block = lax.dynamic_slice_in_dim(all_keys, offset, block_size, 0)
        value_block = lax.dynamic_slice_in_dim(all_values, offset, block_size, 0)
        seg_block = lax.dynamic_slice_in_dim(all_segs, offset, block_size, 0)
        _, key_part, value_part = back_block(key_block, value_block, seg_block, offset)
        return jnp.concatenate([key_part, value_part], axis=1)

    part_rows = lax.map(one_block, jnp.arange(number, dtype=jnp.int32))
    summed = lax.psum_scatter(
        part_rows.reshape(row_count, -1).astype(jnp.bfloat16),
        "ctx",
        scatter_dimension=0,
        tiled=True,
    ).astype(jnp.float32)
    key_sum = summed[:, : local_heads * HEAD_DIM]
    value_sum = summed[:, local_heads * HEAD_DIM :]
    query_grad = (
        query_acc.astype(jnp.bfloat16)
        .transpose(1, 0, 2)
        .reshape(local_rows, local_heads * HEAD_DIM)
    )
    key_grad = key_sum.astype(jnp.bfloat16)
    value_grad = value_sum.astype(jnp.bfloat16)
    running = jnp.einsum("sn,dn->sd", query_grad, w_qkv[0], preferred_element_type=jnp.float32)
    running = running + jnp.einsum(
        "sn,dn->sd", key_grad, w_qkv[1], preferred_element_type=jnp.float32
    )
    normed_grad = lax.psum_scatter(
        (
            running
            + jnp.einsum("sn,dn->sd", value_grad, w_qkv[2], preferred_element_type=jnp.float32)
        ).astype(jnp.bfloat16),
        "head",
        scatter_dimension=0,
        tiled=True,
    ).astype(jnp.float32)
    gain_grad = normed_grad * gain_full
    gradient = (
        readout_own
        + inverse_own * gain_grad
        - state_own * inverse_own**3 * jnp.mean(gain_grad * state_own, axis=-1, keepdims=True)
    )
    return state_own - STEP_SIZE * gradient + jnp.sqrt(2.0 * STEP_SIZE) * noise.astype(jnp.float32)


def solution(mesh):
    placed = (
        P("ctx", None),
        P(),
        P(None, None, "head"),
        P("head", None),
        P("ctx", None),
        P(("ctx", "head"), None),
        P("ctx"),
    )
    return jax.shard_map(
        body, mesh=mesh, in_specs=placed, out_specs=P(("ctx", "head"), None), check_vma=False
    )
```

profile of v0, /device:TPU:11, one launch (start us, length us, event | category | flops | bytes accessed | tf_op | source)
XLA Modules:
  0.0 550.6 jit_solution(13009157587223237203)
XLA Ops:
  10.4 6.9 %fusion.73 = bf16[3,1024,256]{1,2,0:T(8,128)(2,1)S(1)} fusion(bf16[3,2048,256]{2,1,0:T(8,128)(2,1)} %param.15, bf16[1024,2048]{1,0:T(8,128)(2,1)} %param.13, f32[2048]{0:T(1024)S(1)} %convert_element_type.76, f32[1024]{0:T(1024)S(1)} %add_rsqrt_fusion.1), kind=kOutput, calls=%fused_computation.90 | convolution fusion | flops 3230400512 | bytes 8925184 | tf_op jit(solution)/shard_map/sd,cdn->csn/dot_general | solution.py:51
  19.6 6.5 %all_gather.9 = s32[4096]{0:T(1024)S(1)} all-gather(s32[1024]{0:T(1024)S(1)} %copy-done.10), channel_id=1, replica_groups=mesh['ctx'=4,'head'=8] {'ctx'}, dimensions={0}, use_global_device_ids=true | all-gather | bytes 20480 | tf_op jit(solution)/shard_map/all_gather | solution.py:95
  26.1 28.7 %all-gather.5.cloned.1.call-done = bf16[1,4096,256]{1,2,0:T(8,128)(2,1)} async-done(((bf16[1,1024,256]{1,2,0:T(8,128)(2,1)}), bf16[1,4096,256]{1,2,0:T(8,128)(2,1)}) %all-gather.5.cloned.1.call-update) | async-done | bytes 2097168 | tf_op jit(solution)/shard_map/all_gather | solution.py:93
  54.8 4.5 reshape.283
  63.0 28.9 %all-gather.7.cloned.1.call-done = bf16[1,4096,256]{1,2,0:T(8,128)(2,1)} async-done(((bf16[1,1024,256]{1,2,0:T(8,128)(2,1)}), bf16[1,4096,256]{1,2,0:T(8,128)(2,1)}) %all-gather.7.cloned.1.call-update) | async-done | bytes 2097168 | tf_op jit(solution)/shard_map/all_gather | solution.py:94
  91.9 4.5 reshape.284
  96.4 3.6 copy.82
  100.0 83.2 %while.38 = (s32[]{:T(128)}, f32[2,1024]{1,0:T(2,128)S(1)}, f32[2,1024]{1,0:T(2,128)S(1)}, f32[2,1024,128]{2,1,0:T(8,128)}, s32[4]{0:T(128)S(1)}, /*index=5*/s32...) while((s32[]{:T(128)}, f32[2,1024]{1,0:T(2,128)S(1)}, ...), condition=%wide.region_4.5_spmd.clone, body=%wide.region_1.4_spmd.clone.sunk | while | flops 1104949248 | bytes 70942944 | solution.py:35
  104.7 5.1 fusion.158
  109.7 4.7 fusion.160
  115.6 4.4 fusion.162
  124.7 5.1 fusion.158
  129.8 4.7 fusion.160
  135.6 5.4 fusion.162
  145.7 5.1 fusion.158
  150.8 4.7 fusion.160
  156.7 5.4 fusion.162
  166.8 5.1 fusion.158
  171.9 4.7 fusion.160
  177.7 5.4 fusion.162
  190.9 95.9 %all-reduce.2.cloned.1.call-done = bf16[1024,2048]{1,0:T(8,128)(2,1)} async-done(((bf16[1024,2048]{1,0:T(8,128)(2,1)}), bf16[1024,2048]{1,0:T(8,128)(2,1)}) %all-reduce.2.cloned.1.call-update) | async-done | bytes 4194320 | tf_op jit(solution)/shard_map/psum | solution.py:106
  286.9 6.0 %multiply_reduce_fusion = (f32[1024]{0:T(1024)S(1)}, f32[1024]{0:T(1024)S(1)}) fusion(bf16[1024,2048]{1,0:T(8,128)(2,1)} %all-reduce.2.cloned.1.call-done, bf16[1024,2048]{1,0:T(8,128)(2,1)} %param.13, bf16[1024,2048]{1,0:T(8,128)(2,1)} %param.17), kind=kLoop, calls=%fused_computation.77 | loop fusion | flops 16775168 | bytes 12591104 | tf_op jit(solution)/shard_map/reduce_sum | solution.py:15
  305.3 97.3 %while.37 = (s32[]{:T(128)}, bf16[4,1024,512]{2,1,0:T(8,128)(2,1)}, s32[4]{0:T(128)S(1)}, s32[4096]{0:T(1024)S(1)}, s32[1024]{0:T(1024)S(1)}, /*index=5*/bf16[40...) while((s32[]{:T(128)}, bf16[4,1024,512]{2,1,0:T(8,128)(2,1)}, ...), condition=%wide.region_12.13_spmd.clone, body=%wide.region_11.12_spmd.clone.sunk | while | flops 2178418688 | bytes 40952544 | solution.py:168
  309.0 4.5 fusion.151
  313.6 8.0 %fusion.153 = bf16[2,1024,128]{1,2,0:T(8,128)(2,1)S(1)} fusion(bf16[2,1024,128]{1,2,0:T(8,128)(2,1)S(1)} %get-tuple-element.903, f32[2,1024,1024]{2,1,0:T(8,128)} %fusion.151, f32[2,1024]{1,0:T(2,128)S(1)} %get-tuple-element.907, f32[2,1024]{1,0:T(2,128)S(1)} %get-tuple-element.904, pred[1024,1024]{0,1:T(8,128)(4,1)S(1)} %compare_and_fusion.6, ...), kind=kOutput, calls=%fused_computation.17.clone.1 | convolution fusion | flops 1088946176 | bytes 11550720 | tf_op jit(solution)/shard_map/while/body/eval_jaxpr/hqk,hqe->khe/dot_general | solution.py:140
  321.6 6.3 %fusion.152 = bf16[2,1024,128]{1,2,0:T(8,128)(2,1)S(1)} fusion(bf16[2,1024,128]{1,2,0:T(8,128)(2,1)} %get-tuple-element.906, f32[2,1024,1024]{2,1,0:T(8,128)} %fusion.151, f32[2,1024]{1,0:T(2,128)S(1)} %get-tuple-element.904, pred[1024,1024]{0,1:T(8,128)(4,1)S(1)} %compare_and_fusion.6), kind=kOutput, calls=%fused_computation.10.clone.1 | convolution fusion | flops 547356672 | bytes 10493952 | tf_op jit(solution)/shard_map/while/body/eval_jaxpr/hqk,hqe->khe/dot_general | solution.py:136
  333.4 4.5 fusion.151
  337.9 8.0 %fusion.153 = bf16[2,1024,128]{1,2,0:T(8,128)(2,1)S(1)} fusion(bf16[2,1024,128]{1,2,0:T(8,128)(2,1)S(1)} %get-tuple-element.903, f32[2,1024,1024]{2,1,0:T(8,128)} %fusion.151, f32[2,1024]{1,0:T(2,128)S(1)} %get-tuple-element.907, f32[2,1024]{1,0:T(2,128)S(1)} %get-tuple-element.904, pred[1024,1024]{0,1:T(8,128)(4,1)S(1)} %compare_and_fusion.6, ...), kind=kOutput, calls=%fused_computation.17.clone.1 | convolution fusion | flops 1088946176 | bytes 11550720 | tf_op jit(solution)/shard_map/while/body/eval_jaxpr/hqk,hqe->khe/dot_general | solution.py:140
  345.9 6.3 %fusion.152 = bf16[2,1024,128]{1,2,0:T(8,128)(2,1)S(1)} fusion(bf16[2,1024,128]{1,2,0:T(8,128)(2,1)} %get-tuple-element.906, f32[2,1024,1024]{2,1,0:T(8,128)} %fusion.151, f32[2,1024]{1,0:T(2,128)S(1)} %get-tuple-element.904, pred[1024,1024]{0,1:T(8,128)(4,1)S(1)} %compare_and_fusion.6), kind=kOutput, calls=%fused_computation.10.clone.1 | convolution fusion | flops 547356672 | bytes 10493952 | tf_op jit(solution)/shard_map/while/body/eval_jaxpr/hqk,hqe->khe/dot_general | solution.py:136
  357.7 4.5 fusion.151
  362.2 8.0 %fusion.153 = bf16[2,1024,128]{1,2,0:T(8,128)(2,1)S(1)} fusion(bf16[2,1024,128]{1,2,0:T(8,128)(2,1)S(1)} %get-tuple-element.903, f32[2,1024,1024]{2,1,0:T(8,128)} %fusion.151, f32[2,1024]{1,0:T(2,128)S(1)} %get-tuple-element.907, f32[2,1024]{1,0:T(2,128)S(1)} %get-tuple-element.904, pred[1024,1024]{0,1:T(8,128)(4,1)S(1)} %compare_and_fusion.6, ...), kind=kOutput, calls=%fused_computation.17.clone.1 | convolution fusion | flops 1088946176 | bytes 11550720 | tf_op jit(solution)/shard_map/while/body/eval_jaxpr/hqk,hqe->khe/dot_general | solution.py:140
  370.2 6.3 %fusion.152 = bf16[2,1024,128]{1,2,0:T(8,128)(2,1)S(1)} fusion(bf16[2,1024,128]{1,2,0:T(8,128)(2,1)} %get-tuple-element.906, f32[2,1024,1024]{2,1,0:T(8,128)} %fusion.151, f32[2,1024]{1,0:T(2,128)S(1)} %get-tuple-element.904, pred[1024,1024]{0,1:T(8,128)(4,1)S(1)} %compare_and_fusion.6), kind=kOutput, calls=%fused_computation.10.clone.1 | convolution fusion | flops 547356672 | bytes 10493952 | tf_op jit(solution)/shard_map/while/body/eval_jaxpr/hqk,hqe->khe/dot_general | solution.py:136
  382.0 4.5 fusion.151
  386.5 8.0 %fusion.153 = bf16[2,1024,128]{1,2,0:T(8,128)(2,1)S(1)} fusion(bf16[2,1024,128]{1,2,0:T(8,128)(2,1)S(1)} %get-tuple-element.903, f32[2,1024,1024]{2,1,0:T(8,128)} %fusion.151, f32[2,1024]{1,0:T(2,128)S(1)} %get-tuple-element.907, f32[2,1024]{1,0:T(2,128)S(1)} %get-tuple-element.904, pred[1024,1024]{0,1:T(8,128)(4,1)S(1)} %compare_and_fusion.6, ...), kind=kOutput, calls=%fused_computation.17.clone.1 | convolution fusion | flops 1088946176 | bytes 11550720 | tf_op jit(solution)/shard_map/while/body/eval_jaxpr/hqk,hqe->khe/dot_general | solution.py:140
  394.5 6.3 %fusion.152 = bf16[2,1024,128]{1,2,0:T(8,128)(2,1)S(1)} fusion(bf16[2,1024,128]{1,2,0:T(8,128)(2,1)} %get-tuple-element.906, f32[2,1024,1024]{2,1,0:T(8,128)} %fusion.151, f32[2,1024]{1,0:T(2,128)S(1)} %get-tuple-element.904, pred[1024,1024]{0,1:T(8,128)(4,1)S(1)} %compare_and_fusion.6), kind=kOutput, calls=%fused_computation.10.clone.1 | convolution fusion | flops 547356672 | bytes 10493952 | tf_op jit(solution)/shard_map/while/body/eval_jaxpr/hqk,hqe->khe/dot_general | solution.py:136
  402.7 71.2 %while.39 = (s32[]{:T(128)}, f32[2,1024,128]{2,1,0:T(8,128)}, s32[4]{0:T(128)S(1)}, s32[4,1024]{1,0:T(4,128)S(1)}, s32[1024]{0:T(1024)S(1)}, /*index=5*/bf16[4,1...) while((s32[]{:T(128)}, f32[2,1024,128]{2,1,0:T(8,128)}, ...), condition=%wide.region_10.11_spmd.clone, body=%wide.region_9.10_spmd.clone.sunk | while | flops 1629227008 | bytes 27836616 | solution.py:35
  406.6 4.8 fusion.169
  411.4 9.0 %fusion.170 = f32[2,1024,128]{2,1,0:T(8,128)} fusion(bf16[1024,2,128]{0,2,1:T(8,128)(2,1)S(1)} %bitcast.223, f32[2,1024,1024]{2,1,0:T(8,128)} %fusion.169, f32[2,1024]{1,0:T(2,128)S(1)} %get-tuple-element.861, f32[2,1024]{1,0:T(2,128)S(1)} %get-tuple-element.858, pred[1024,1024]{0,1:T(8,128)(4,1)S(1)} %compare_and_fusion.8, ...), kind=kOutput, calls=%fused_computation.63.clone.1 | convolution fusion | flops 1089208320 | bytes 13123585 | tf_op jit(solution)/shard_map/while/body/eval_jaxpr/hqk,khe->hqe/dot_general | solution.py:144
  424.3 4.5 fusion.169
  428.8 9.4 %fusion.170 = f32[2,1024,128]{2,1,0:T(8,128)} fusion(bf16[1024,2,128]{0,2,1:T(8,128)(2,1)S(1)} %bitcast.223, f32[2,1024,1024]{2,1,0:T(8,128)} %fusion.169, f32[2,1024]{1,0:T(2,128)S(1)} %get-tuple-element.861, f32[2,1024]{1,0:T(2,128)S(1)} %get-tuple-element.858, pred[1024,1024]{0,1:T(8,128)(4,1)S(1)} %compare_and_fusion.8, ...), kind=kOutput, calls=%fused_computation.63.clone.1 | convolution fusion | flops 1089208320 | bytes 13123585 | tf_op jit(solution)/shard_map/while/body/eval_jaxpr/hqk,khe->hqe/dot_general | solution.py:144
  442.2 4.5 fusion.169
  446.8 9.4 %fusion.170 = f32[2,1024,128]{2,1,0:T(8,128)} fusion(bf16[1024,2,128]{0,2,1:T(8,128)(2,1)S(1)} %bitcast.223, f32[2,1024,1024]{2,1,0:T(8,128)} %fusion.169, f32[2,1024]{1,0:T(2,128)S(1)} %get-tuple-element.861, f32[2,1024]{1,0:T(2,128)S(1)} %get-tuple-element.858, pred[1024,1024]{0,1:T(8,128)(4,1)S(1)} %compare_and_fusion.8, ...), kind=kOutput, calls=%fused_computation.63.clone.1 | convolution fusion | flops 1089208320 | bytes 13123585 | tf_op jit(solution)/shard_map/while/body/eval_jaxpr/hqk,khe->hqe/dot_general | solution.py:144
  459.9 4.5 fusion.169
  464.4 9.3 %fusion.170 = f32[2,1024,128]{2,1,0:T(8,128)} fusion(bf16[1024,2,128]{0,2,1:T(8,128)(2,1)S(1)} %bitcast.223, f32[2,1024,1024]{2,1,0:T(8,128)} %fusion.169, f32[2,1024]{1,0:T(2,128)S(1)} %get-tuple-element.861, f32[2,1024]{1,0:T(2,128)S(1)} %get-tuple-element.858, pred[1024,1024]{0,1:T(8,128)(4,1)S(1)} %compare_and_fusion.8, ...), kind=kOutput, calls=%fused_computation.63.clone.1 | convolution fusion | flops 1089208320 | bytes 13123585 | tf_op jit(solution)/shard_map/while/body/eval_jaxpr/hqk,khe->hqe/dot_general | solution.py:144
  475.3 5.8 %fusion.85 = f32[1024,2048]{1,0:T(8,128)} fusion(bf16[1024,256]{0,1:T(8,128)(2,1)S(1)} %bitcast.238, bf16[3,2048,256]{2,1,0:T(8,128)(2,1)} %param.15), kind=kOutput, calls=%fused_computation.96 | convolution fusion | flops 1073741824 | bytes 9961472 | tf_op jit(solution)/shard_map/sn,dn->sd/dot_general | solution.py:184
  485.2 4.7 add_convert_fusion
  489.9 6.6 %convert_element_type.75 = f32[1024,2048]{1,0:T(8,128)} convert(bf16[1024,2048]{1,0:T(8,128)(2,1)} %param.13) | non-fusion elementwise | flops 2097152 | bytes 12582912 | tf_op jit(solution)/shard_map/convert_element_type | solution.py:47
  497.3 41.7 %reduce-scatter.5.cloned.1.call-done = bf16[128,2048]{1,0:T(8,128)(2,1)} async-done(((bf16[1024,2048]{1,0:T(8,128)(2,1)}), bf16[128,2048]{1,0:T(8,128)(2,1)}) %reduce-scatter.5.cloned.1.call-update) | async-done | bytes 524304 | tf_op jit(solution)/shard_map/reduce_scatter | solution.py:188
  (173 shorter events, 98.5 us)
Async XLA Ops:
  6.5 180.5 %copy-start = (bf16[256,2048]{1,0:T(8,128)(2,1)S(1)}, bf16[256,2048]{1,0:T(8,128)(2,1)}, u32[]{:S(2)}) copy-start(bf16[256,2048]{1,0:T(8,128)(2,1)} %param.16) | copy-start | bytes 3145732
  6.5 48.3 %all-gather.5.cloned.1.call-start = ((), (), s32[]{:S(2)}) async-start(), calls=%async_computation.5 | async-start | bytes 2621440 | tf_op jit(solution)/shard_map/all_gather | solution.py:93
  7.3 10.0 %copy-start.13 = (f32[2048]{0:T(1024)}, f32[2048]{0:T(1024)S(1)}, u32[]{:S(2)}) copy-start(f32[2048]{0:T(1024)S(1)} %convert_element_type.76) | copy-start | bytes 24580
  10.4 7.0 %copy-start.15 = (f32[1024]{0:T(1024)}, f32[1024]{0:T(1024)S(1)}, u32[]{:S(2)}) copy-start(f32[1024]{0:T(1024)S(1)} %add_rsqrt_fusion.1) | copy-start | bytes 12292
  10.4 9.2 %copy-start.10 = (s32[1024]{0:T(1024)S(1)}, s32[1024]{0:T(1024)}, u32[]{:S(2)}) copy-start(s32[1024]{0:T(1024)} %param.19) | copy-start | bytes 12292
  18.5 73.4 %all-gather.7.cloned.1.call-start = ((), (), s32[]{:S(2)}) async-start(), calls=%async_computation.6 | async-start | bytes 2621440 | tf_op jit(solution)/shard_map/all_gather | solution.py:94
  19.3 267.6 %all-reduce.2.cloned.1.call-start = ((), (), s32[]{:S(2)}) async-start(), calls=%async_computation.2 | async-start | bytes 8388608 | tf_op jit(solution)/shard_map/psum | solution.py:106
  109.7 5.8 %copy-start.2 = (f32[2,1024,1024]{2,1,0:T(8,128)S(1)}, f32[2,1024,1024]{2,1,0:T(8,128)}, u32[]{:S(2)}) copy-start(f32[2,1024,1024]{2,1,0:T(8,128)} %get-tuple-element.764) | copy-start | bytes 25165828 | tf_op jit(solution)/shard_map/while
  109.7 5.9 %copy-start.8 = (bf16[1,1024,256]{1,2,0:T(8,128)(2,1)S(1)}, bf16[1,1024,256]{1,2,0:T(8,128)(2,1)}, u32[]{:S(2)}) copy-start(bf16[1,1024,256]{1,2,0:T(8,128)(2,1)} %get-tuple-element.766) | copy-start | bytes 1572868 | tf_op jit(solution)/shard_map/while
  129.7 5.8 %copy-start.2 = (f32[2,1024,1024]{2,1,0:T(8,128)S(1)}, f32[2,1024,1024]{2,1,0:T(8,128)}, u32[]{:S(2)}) copy-start(f32[2,1024,1024]{2,1,0:T(8,128)} %get-tuple-element.764) | copy-start | bytes 25165828 | tf_op jit(solution)/shard_map/while
  129.7 5.9 %copy-start.8 = (bf16[1,1024,256]{1,2,0:T(8,128)(2,1)S(1)}, bf16[1,1024,256]{1,2,0:T(8,128)(2,1)}, u32[]{:S(2)}) copy-start(bf16[1,1024,256]{1,2,0:T(8,128)(2,1)} %get-tuple-element.766) | copy-start | bytes 1572868 | tf_op jit(solution)/shard_map/while
  150.8 5.8 %copy-start.2 = (f32[2,1024,1024]{2,1,0:T(8,128)S(1)}, f32[2,1024,1024]{2,1,0:T(8,128)}, u32[]{:S(2)}) copy-start(f32[2,1024,1024]{2,1,0:T(8,128)} %get-tuple-element.764) | copy-start | bytes 25165828 | tf_op jit(solution)/shard_map/while
  150.8 5.9 %copy-start.8 = (bf16[1,1024,256]{1,2,0:T(8,128)(2,1)S(1)}, bf16[1,1024,256]{1,2,0:T(8,128)(2,1)}, u32[]{:S(2)}) copy-start(bf16[1,1024,256]{1,2,0:T(8,128)(2,1)} %get-tuple-element.766) | copy-start | bytes 1572868 | tf_op jit(solution)/shard_map/while
  171.9 5.8 %copy-start.2 = (f32[2,1024,1024]{2,1,0:T(8,128)S(1)}, f32[2,1024,1024]{2,1,0:T(8,128)}, u32[]{:S(2)}) copy-start(f32[2,1024,1024]{2,1,0:T(8,128)} %get-tuple-element.764) | copy-start | bytes 25165828 | tf_op jit(solution)/shard_map/while
  171.9 5.9 %copy-start.8 = (bf16[1,1024,256]{1,2,0:T(8,128)(2,1)S(1)}, bf16[1,1024,256]{1,2,0:T(8,128)(2,1)}, u32[]{:S(2)}) copy-start(bf16[1,1024,256]{1,2,0:T(8,128)(2,1)} %get-tuple-element.766) | copy-start | bytes 1572868 | tf_op jit(solution)/shard_map/while
  190.3 290.8 %reduce-scatter.3.cloned.1.call-start = ((), (), s32[]{:S(2)}) async-start(), calls=%async_computation.3 | async-start | bytes 5242880 | tf_op jit(solution)/shard_map/reduce_scatter | solution.py:169
  286.9 6.0 %copy-start.3 = (bf16[1024,2048]{1,0:T(8,128)(2,1)S(1)}, bf16[1024,2048]{1,0:T(8,128)(2,1)}, u32[]{:S(2)}) copy-start(bf16[1024,2048]{1,0:T(8,128)(2,1)} %param.13) | copy-start | bytes 12582916
  286.9 7.1 %copy-start.6 = (bf16[1024,2048]{1,0:T(8,128)(2,1)S(1)}, bf16[1024,2048]{1,0:T(8,128)(2,1)}, u32[]{:S(2)}) copy-start(bf16[1024,2048]{1,0:T(8,128)(2,1)} %param.17) | copy-start | bytes 12582916
  286.9 8.3 %copy-start.7 = (bf16[1024,2048]{1,0:T(8,128)(2,1)S(1)}, bf16[1024,2048]{1,0:T(8,128)(2,1)}, u32[]{:S(2)}) copy-start(bf16[1024,2048]{1,0:T(8,128)(2,1)} %all-reduce.2.cloned.1.call-done) | copy-start | bytes 12582916
  297.8 3.2 copy-start.5
  402.6 136.4 %reduce-scatter.5.cloned.1.call-start = ((), (), s32[]{:S(2)}) async-start(), calls=%async_computation.4 | async-start | bytes 4718592 | tf_op jit(solution)/shard_map/reduce_scatter | solution.py:188
  402.9 8.6 %copy-start.11 = (bf16[2,1024,128]{2,1,0:T(8,128)(2,1)S(1)}, bf16[2,1024,128]{2,1,0:T(8,128)(2,1)}, u32[]{:S(2)}) copy-start(bf16[2,1024,128]{2,1,0:T(8,128)(2,1)} %get-tuple-element.860) | copy-start | bytes 1572868 | tf_op jit(solution)/shard_map/while
  420.5 8.3 %copy-start.11 = (bf16[2,1024,128]{2,1,0:T(8,128)(2,1)S(1)}, bf16[2,1024,128]{2,1,0:T(8,128)(2,1)}, u32[]{:S(2)}) copy-start(bf16[2,1024,128]{2,1,0:T(8,128)(2,1)} %get-tuple-element.860) | copy-start | bytes 1572868 | tf_op jit(solution)/shard_map/while
  438.2 8.6 %copy-start.11 = (bf16[2,1024,128]{2,1,0:T(8,128)(2,1)S(1)}, bf16[2,1024,128]{2,1,0:T(8,128)(2,1)}, u32[]{:S(2)}) copy-start(bf16[2,1024,128]{2,1,0:T(8,128)(2,1)} %get-tuple-element.860) | copy-start | bytes 1572868 | tf_op jit(solution)/shard_map/while
  456.1 8.3 %copy-start.11 = (bf16[2,1024,128]{2,1,0:T(8,128)(2,1)S(1)}, bf16[2,1024,128]{2,1,0:T(8,128)(2,1)}, u32[]{:S(2)}) copy-start(bf16[2,1024,128]{2,1,0:T(8,128)(2,1)} %get-tuple-element.860) | copy-start | bytes 1572868 | tf_op jit(solution)/shard_map/while
  481.1 3.9 copy-start.4
  481.1 4.1 copy-start.9
  489.9 49.1 %copy-start.14 = (f32[2048]{0:T(1024)S(1)}, f32[2048]{0:T(1024)}, u32[]{:S(2)}) copy-start(f32[2048]{0:T(1024)} %copy-done.13) | copy-start | bytes 24580
  489.9 50.7 %copy-start.12 = (bf16[128,2048]{1,0:T(8,128)(2,1)S(1)}, bf16[128,2048]{1,0:T(8,128)(2,1)}, u32[]{:S(2)}) copy-start(bf16[128,2048]{1,0:T(8,128)(2,1)} %param.18) | copy-start | bytes 1572868
  489.9 53.9 %copy-start.1 = (bf16[256,2048]{1,0:T(8,128)(2,1)S(1)}, bf16[256,2048]{1,0:T(8,128)(2,1)}, u32[]{:S(2)}) copy-start(bf16[256,2048]{1,0:T(8,128)(2,1)} %param.16) | copy-start | bytes 3145732
Sparse Core Ops, SparseCore 0:
  18.6 36.1 all-gather.4
  56.7 35.1 all-gather.6
  190.5 96.3 all-reduce.1
  402.7 52.7 reduce-scatter.2
  490.0 48.9 reduce-scatter.4
where the time goes:
time: 559 us; the launch traced here: 551 us
  matrix products  198 us (35%)
  waiting for transfers between devices  196 us (35%)
  local copies, waits for them, and re-layouts  68 us (12%)
  other arithmetic  64.9 us (12%)
  between operations  13.6 us (2%)
  blocking collectives  6.47 us (1%)
    psum x1, waiting for transfers between devices, body(): lax.psum(term.astype(jnp.bfloat16), 'head').astype(jnp.float32)  95.9 us
    reduce_scatter x1, waiting for transfers between devices, body(): lax.psum_scatter((running + jnp.einsum('sn,dn->sd', value_grad, w_qkv[2],...  41.7 us
    dot_general x4, matrix products, back_block(): jnp.einsum('hqk,khe->hqe', dscore_half, key_heads, preferred_element_type...  37.1 us
    dot_general x8, matrix products, back_block(): jnp.einsum('hqe,khe->hqk', queries, key_heads, preferred_element_type=jnp...  36.6 us
    dot_general x4, matrix products, back_block(): jnp.einsum('hqk,hqe->khe', dscore_half, queries, preferred_element_type=j...  32 us
    all_gather x1, waiting for transfers between devices, body(): lax.all_gather(value_rows, 'ctx', axis=0, tiled=True)  28.9 us
    all_gather x1, waiting for transfers between devices, body(): lax.all_gather(key_rows, 'ctx', axis=0, tiled=True)  28.7 us
    dot_general x4, matrix products, back_block(): jnp.einsum('hqk,hqe->khe', prob_half, grads_out, preferred_element_type=j...  25.3 us
  transfers between devices with their start and end apart: 5, of which 4 were waited for; matrix products, arithmetic and copies ran while one was open for 17% of the time, Pallas kernels for 0%

commit v1 on v0

v1 whole, which is shorter than its diff:
```python
import functools

import jax
import jax.numpy as jnp
from jax import lax
from jax.experimental import pallas as pl
from jax.experimental.pallas import tpu as pltpu
from jax.sharding import PartitionSpec as P

HEAD_DIM = 128
EPSILON = 1e-05
STEP_SIZE = 0.25
NEGATIVE = -1e30
LOG2E = 1.4426950408889634
MESH = pl.DeviceIdType.MESH
VMEM = pl.BlockSpec(memory_space=pltpu.VMEM)
ANY = pl.BlockSpec(memory_space=pl.ANY)
NT = (((1,), (1,)), ((), ()))
TN = (((0,), (0,)), ((), ()))
FORWARD_BLOCKS = (256, 512)
BACKWARD_BLOCKS = (256, 512)


def row_scale(matrix):
    return lax.rsqrt(jnp.mean(matrix * matrix, axis=-1, keepdims=True) + EPSILON)


def dot32(left, right, dims):
    return lax.dot_general(left, right, dims, preferred_element_type=jnp.float32)


def greet(axis, number, me):
    barrier = pltpu.get_barrier_semaphore()
    for step in range(1, number):
        pl.semaphore_signal(
            barrier, inc=1, device_id={axis: lax.rem(me + step, number)}, device_id_type=MESH
        )
    pl.semaphore_wait(barrier, number - 1)


def gather_kernel(
    number, key_ref, value_ref, seg_ref, keys, values, segs, send_sem, recv_sem, own_sem
):
    me = lax.axis_index("ctx")
    rows = key_ref.shape[0]
    greet("ctx", number, me)
    mine = pl.ds(pl.multiple_of(me * rows, rows), rows)
    pairs = (
        (key_ref, keys.at[mine]),
        (value_ref, values.at[mine]),
        (seg_ref, segs.at[me]),
    )
    copies = []
    for step in range(1, number):
        for index, (source, target) in enumerate(pairs):
            copy = pltpu.make_async_remote_copy(
                src_ref=source,
                dst_ref=target,
                send_sem=send_sem.at[step, index],
                recv_sem=recv_sem.at[step, index],
                device_id={"ctx": lax.rem(me + step, number)},
                device_id_type=MESH,
            )
            copy.start()
            copies.append(copy)
    for index, (source, target) in enumerate(pairs):
        copy = pltpu.make_async_copy(source, target, own_sem.at[index])
        copy.start()
        copies.append(copy)
    for copy in copies:
        copy.wait()


def gather_keys(number, key_rows, value_rows, segment_ids):
    rows, width = key_rows.shape
    seg = segment_ids.reshape(-1, 128)
    full = jax.ShapeDtypeStruct((number * rows, width), key_rows.dtype)
    keys, values, segs = pl.pallas_call(
        functools.partial(gather_kernel, number),
        out_shape=(full, full, jax.ShapeDtypeStruct((number,) + seg.shape, seg.dtype)),
        in_specs=[VMEM] * 3,
        out_specs=(ANY,) * 3,
        scratch_shapes=[
            pltpu.SemaphoreType.DMA((number, 3)),
            pltpu.SemaphoreType.DMA((number, 3)),
            pltpu.SemaphoreType.DMA((3,)),
        ],
        compiler_params=pltpu.CompilerParams(collective_id=0, has_side_effects=True),
    )(key_rows, value_rows, seg)
    return keys, values, segs.reshape(-1)


def block_ranges(table, index):
    return [table[index, column] for column in range(4)]


def forward_kernel(
    heads, bq, bk, table, query_ref, key_ref, value_ref, start_ref, pos_ref, out_ref, log_ref
):
    factor = HEAD_DIM ** (-0.5) * LOG2E
    blocks = query_ref.shape[0] // bq

    def one_block(index, _):
        low, inner_low, inner_high, high = block_ranges(table, index)
        rows = pl.ds(pl.multiple_of(index * bq, bq), bq)
        start, pos = start_ref[index], pos_ref[index]

        def step(masked, piece, carry):
            keys_at = pl.ds(pl.multiple_of(piece * bk, bk), bk)
            if masked:
                key_pos = piece * bk + lax.broadcasted_iota(jnp.int32, (bk, bq), 0)
                allowed = (key_pos >= start) & (key_pos <= pos)
            result = []
            for head in range(heads):
                top, total, acc = carry[head]
                cols = pl.ds(head * HEAD_DIM, HEAD_DIM)
                scores = dot32(key_ref[keys_at, cols], query_ref[rows, cols], NT)
                if masked:
                    scores = jnp.where(allowed, scores, NEGATIVE)
                new_top = jnp.maximum(top, jnp.max(scores, axis=0, keepdims=True) * factor)
                weights = jnp.exp2(scores * factor - new_top)
                scale = jnp.exp2(top - new_top)
                total = total * scale + jnp.sum(weights, axis=0, keepdims=True)
                acc = acc * scale + dot32(
                    value_ref[keys_at, cols], weights.astype(jnp.bfloat16), TN
                )
                result.append((new_top, total, acc))
            return tuple(result)

        carry = tuple(
            (
                jnp.full((1, bq), NEGATIVE, jnp.float32),
                jnp.zeros((1, bq), jnp.float32),
                jnp.zeros((HEAD_DIM, bq), jnp.float32),
            )
            for _ in range(heads)
        )
        carry = lax.fori_loop(low, inner_low, functools.partial(step, True), carry)
        carry = lax.fori_loop(inner_low, inner_high, functools.partial(step, False), carry)
        carry = lax.fori_loop(inner_high, high, functools.partial(step, True), carry)
        for head in range(heads):
            top, total, acc = carry[head]
            out_ref[rows, pl.ds(head * HEAD_DIM, HEAD_DIM)] = (acc / total).T.astype(jnp.bfloat16)
            log_ref[index, pl.ds(head, 1), :] = top + jnp.log2(total)
        return 0

    lax.fori_loop(0, blocks, one_block, 0)


def backward_kernel(
    heads, bq, bk, table, query_ref, key_ref, value_ref, grad_ref, out_ref, log_ref, start_ref,
    pos_ref, query_out, pair_out, pair_acc,
):
    score_scale = HEAD_DIM ** (-0.5)
    factor = score_scale * LOG2E
    blocks = query_ref.shape[0] // bq
    width = heads * HEAD_DIM
    pair_rows = pair_acc.shape[0]

    def clear(piece, _):
        at = pl.ds(pl.multiple_of(piece * bk, bk), bk)
        pair_acc[at, :] = jnp.zeros((bk, 2 * width), jnp.float32)
        return 0

    lax.fori_loop(0, pair_rows // bk, clear, 0)

    def one_block(index, _):
        low, inner_low, inner_high, high = block_ranges(table, index)
        rows = pl.ds(pl.multiple_of(index * bq, bq), bq)
        start, pos = start_ref[index], pos_ref[index]
        deltas, logs = [], []
        for head in range(heads):
            cols = pl.ds(head * HEAD_DIM, HEAD_DIM)
            product = grad_ref[rows, cols].astype(jnp.float32) * out_ref[rows, cols].astype(
                jnp.float32
            )
            deltas.append(jnp.sum(product.T, axis=0, keepdims=True))
            logs.append(log_ref[index, pl.ds(head, 1), :])

        def step(masked, piece, carry):
            keys_at = pl.ds(pl.multiple_of(piece * bk, bk), bk)
            if masked:
                key_pos = piece * bk + lax.broadcasted_iota(jnp.int32, (bk, bq), 0)
                allowed = (key_pos >= start) & (key_pos <= pos)
            result = []
            for head in range(heads):
                cols = pl.ds(head * HEAD_DIM, HEAD_DIM)
                value_cols = pl.ds(width + head * HEAD_DIM, HEAD_DIM)
                key_block, query_block = key_ref[keys_at, cols], query_ref[rows, cols]
                grad_block = grad_ref[rows, cols]
                scores = dot32(key_block, query_block, NT)
                probabilities = jnp.exp2(scores * factor - logs[head])
                if masked:
                    probabilities = jnp.where(allowed, probabilities, 0.0)
                dprobs = dot32(value_ref[keys_at, cols], grad_block, NT)
                dscores = (probabilities * (dprobs - deltas[head])).astype(jnp.bfloat16)
                pair_acc[keys_at, value_cols] += jnp.dot(
                    probabilities.astype(jnp.bfloat16),
                    grad_block,
                    preferred_element_type=jnp.float32,
                )
                pair_acc[keys_at, cols] += jnp.dot(
                    dscores, query_block, preferred_element_type=jnp.float32
                )
                result.append(carry[head] + dot32(key_block, dscores, TN))
            return tuple(result)

        carry = tuple(jnp.zeros((HEAD_DIM, bq), jnp.float32) for _ in range(heads))
        carry = lax.fori_loop(low, inner_low, functools.partial(step, True), carry)
        carry = lax.fori_loop(inner_low, inner_high, functools.partial(step, False), carry)
        carry = lax.fori_loop(inner_high, high, functools.partial(step, True), carry)
        for head in range(heads):
            query_out[rows, pl.ds(head * HEAD_DIM, HEAD_DIM)] = (
                carry[head].T * score_scale
            ).astype(jnp.bfloat16)
        return 0

    lax.fori_loop(0, blocks, one_block, 0)

    def flush(piece, _):
        at = pl.ds(pl.multiple_of(piece * bk, bk), bk)
        pair_out[at, :width] = (pair_acc[at, :width] * score_scale).astype(jnp.bfloat16)
        pair_out[at, width:] = pair_acc[at, width:].astype(jnp.bfloat16)
        return 0

    lax.fori_loop(0, pair_rows // bk, flush, 0)


def make_table(start, pos, bq, bk):
    starts, places = start.reshape(-1, bq), pos.reshape(-1, bq)
    low = starts[:, 0] // bk
    inner_low = (starts[:, -1] + bk - 1) // bk
    inner_high = jnp.maximum(inner_low, (places[:, 0] + 1) // bk)
    high = places[:, -1] // bk + 1
    return jnp.stack([low, inner_low, inner_high, high], axis=1).astype(jnp.int32)


def middle_kernel(
    number, part_ref, w_any, state_ref, probe_ref, grad_out, readout_out, w_ref, joined, half,
    sending, landing, send_sem, recv_sem, back_send, back_recv, w_sem,
):
    me = lax.axis_index("head")
    width = part_ref.shape[1]
    own = state_ref.shape[0]
    model = state_ref.shape[1]
    w_copy = pltpu.make_async_copy(w_any, w_ref, w_sem)
    w_copy.start()
    greet("head", number, me)
    my_cols = pl.ds(pl.multiple_of(me * width, width), width)
    my_rows = pl.ds(pl.multiple_of(me * own, own), own)
    copies = []
    for step in range(1, number):
        peer = lax.rem(me + step, number)
        copy = pltpu.make_async_remote_copy(
            src_ref=part_ref.at[pl.ds(pl.multiple_of(peer * own, own), own)],
            dst_ref=joined.at[:, my_cols],
            send_sem=send_sem.at[step],
            recv_sem=recv_sem.at[step],
            device_id={"head": peer},
            device_id_type=MESH,
        )
        copy.start()
        copies.append(copy)
    joined[:, my_cols] = part_ref[my_rows, :]
    w_copy.wait()
    for copy in copies:
        copy.wait()

    tile = min(256, model)

    def project(piece, carry):
        squares, products = carry
        cols = pl.ds(pl.multiple_of(piece * tile, tile), tile)
        layer = state_ref[:, cols].astype(jnp.float32) + jnp.dot(
            joined[...], w_ref[:, cols], preferred_element_type=jnp.float32
        )
        readout_out[:, cols] = layer
        squares = squares + jnp.sum(layer * layer, axis=1, keepdims=True)
        products = products + jnp.sum(
            layer * probe_ref[:, cols].astype(jnp.float32), axis=1, keepdims=True
        )
        return squares, products

    zero = jnp.zeros((own, 1), jnp.float32)
    squares, products = lax.fori_loop(0, model // tile, project, (zero, zero))
    scale = lax.rsqrt(squares / model + EPSILON)
    bend = scale**3 * (products / model)

    def finish(piece, _):
        cols = pl.ds(pl.multiple_of(piece * tile, tile), tile)
        readout = scale * probe_ref[:, cols].astype(jnp.float32) - readout_out[:, cols] * bend
        readout_out[:, cols] = readout
        half[:, cols] = readout.astype(jnp.bfloat16)
        return 0

    lax.fori_loop(0, model // tile, finish, 0)
    copies = []
    for step in range(1, number):
        peer = lax.rem(me + step, number)
        sending[step] = dot32(
            half[...], w_ref[pl.ds(pl.multiple_of(peer * width, width), width), :], NT
        ).astype(jnp.bfloat16)
        copy = pltpu.make_async_remote_copy(
            src_ref=sending.at[step],
            dst_ref=landing.at[my_rows],
            send_sem=back_send.at[step],
            recv_sem=back_recv.at[step],
            device_id={"head": peer},
            device_id_type=MESH,
        )
        copy.start()
        copies.append(copy)
    landing[my_rows, :] = dot32(half[...], w_ref[my_cols, :], NT).astype(jnp.bfloat16)
    for copy in copies:
        copy.wait()
    grad_out[...] = landing[...]


def middle(number, part, w_full, state_own, probe_own):
    rows, width = part.shape
    own, model = state_own.shape
    return pl.pallas_call(
        functools.partial(middle_kernel, number),
        out_shape=(
            jax.ShapeDtypeStruct((rows, width), jnp.bfloat16),
            jax.ShapeDtypeStruct((own, model), jnp.float32),
        ),
        in_specs=[VMEM, ANY, VMEM, VMEM],
        out_specs=(VMEM, VMEM),
        scratch_shapes=[
            pltpu.VMEM(w_full.shape, jnp.bfloat16),
            pltpu.VMEM((own, number * width), jnp.bfloat16),
            pltpu.VMEM((own, model), jnp.bfloat16),
            pltpu.VMEM((number, own, width), jnp.bfloat16),
            pltpu.VMEM((rows, width), jnp.bfloat16),
            pltpu.SemaphoreType.DMA((number,)),
            pltpu.SemaphoreType.DMA((number,)),
            pltpu.SemaphoreType.DMA((number,)),
            pltpu.SemaphoreType.DMA((number,)),
            pltpu.SemaphoreType.DMA,
        ],
        compiler_params=pltpu.CompilerParams(
            collective_id=1, has_side_effects=True, vmem_limit_bytes=60 * 2**20
        ),
    )(part, w_full, state_own, probe_own)


def tail_kernel(
    ctx_count, number, pair_any, query_ref, w_ref, sum_out, own_pair, arriving, gathered, terms,
    from_partner, reduced, landing, ctx_send, ctx_recv, p_send, p_recv, z_send, z_recv, own_sem,
):
    ctx, me = lax.axis_index("ctx"), lax.axis_index("head")
    groups = number // 2
    group, core = me // 2, lax.rem(me, 2)
    partner = group * 2 + 1 - core
    rows, width = query_ref.shape
    own, model = sum_out.shape
    chunk = 2 * own
    own_copy = pltpu.make_async_copy(
        pair_any.at[pl.ds(pl.multiple_of(ctx * rows, rows), rows)], own_pair, own_sem
    )
    own_copy.start()
    barrier = pltpu.get_barrier_semaphore()
    peers = [{"ctx": lax.rem(ctx + step, ctx_count)} for step in range(1, ctx_count)]
    peers.append({"head": partner})
    for step in range(1, groups):
        peers.append({"head": lax.rem(group + step, groups) * 2 + core})
    for peer in peers:
        pl.semaphore_signal(barrier, inc=1, device_id=peer, device_id_type=MESH)
    pl.semaphore_wait(barrier, len(peers))

    def chunk_start(order):
        dest = lax.rem(group + order + 1, groups)
        return dest, pl.multiple_of(dest * chunk, chunk)

    def ctx_copy(order, step):
        target = lax.rem(ctx - step + ctx_count, ctx_count)
        _, first = chunk_start(order)
        return pltpu.make_async_remote_copy(
            src_ref=pair_any.at[pl.ds(pl.multiple_of(target * rows + first, chunk), chunk)],
            dst_ref=arriving.at[order, step - 1],
            send_sem=ctx_send.at[order, step],
            recv_sem=ctx_recv.at[order, step],
            device_id={"ctx": target},
            device_id_type=MESH,
        )

    for order in range(groups):
        for step in range(1, ctx_count):

            @pl.when(step <= ctx)
            def _():
                ctx_copy(order, step).start()

    own_copy.wait()
    tile = min(512, model)
    mine = pl.ds(pl.multiple_of(core * own, own), own)
    theirs = pl.ds(pl.multiple_of((1 - core) * own, own), own)
    waiting = []
    for order in range(groups):
        dest, first = chunk_start(order)
        at = pl.ds(first, chunk)
        gathered[...] = own_pair[at, :].astype(jnp.float32)
        for step in range(1, ctx_count):

            @pl.when(ctx + step < ctx_count)
            def _():
                ctx_copy(order, step).wait_recv()
                gathered[...] += arriving[order, step - 1].astype(jnp.float32)

        def multiply(piece, _):
            cols = pl.ds(pl.multiple_of(piece * tile, tile), tile)
            term = dot32(query_ref[at, :], w_ref[0, cols, :], NT)
            term += dot32(gathered[:, :width].astype(jnp.bfloat16), w_ref[1, cols, :], NT)
            term += dot32(gathered[:, width:].astype(jnp.bfloat16), w_ref[2, cols, :], NT)
            terms[order, :, cols] = term.astype(jnp.bfloat16)
            return 0

        lax.fori_loop(0, model // tile, multiply, 0)
        copy = pltpu.make_async_remote_copy(
            src_ref=terms.at[order, theirs],
            dst_ref=from_partner.at[order],
            send_sem=p_send.at[order],
            recv_sem=p_recv.at[order],
            device_id={"head": partner},
            device_id_type=MESH,
        )
        copy.start()
        copy.wait()
        both = terms[order, mine, :].astype(jnp.float32) + from_partner[order].astype(jnp.float32)
        if order < groups - 1:
            reduced[order] = both.astype(jnp.bfloat16)
            copy = pltpu.make_async_remote_copy(
                src_ref=reduced.at[order],
                dst_ref=landing.at[order],
                send_sem=z_send.at[order],
                recv_sem=z_recv.at[order],
                device_id={"head": dest * 2 + core},
                device_id_type=MESH,
            )
            copy.start()
            waiting.append(copy)
        else:
            sum_out[...] = both
    for order, copy in enumerate(waiting):
        copy.wait()
        sum_out[...] += landing[order].astype(jnp.float32)
    for order in range(groups):
        for step in range(1, ctx_count):

            @pl.when(step <= ctx)
            def _():
                ctx_copy(order, step).wait_send()


def tail(ctx_count, number, pair, query_grad, w_qkv):
    rows, width = query_grad.shape
    model = w_qkv.shape[1]
    own, groups = rows // number, number // 2
    half, full = jnp.bfloat16, jnp.float32
    dma = pltpu.SemaphoreType.DMA
    return pl.pallas_call(
        functools.partial(tail_kernel, ctx_count, number),
        out_shape=jax.ShapeDtypeStruct((own, model), full),
        in_specs=[ANY, VMEM, VMEM],
        out_specs=VMEM,
        scratch_shapes=[
            pltpu.VMEM((rows, 2 * width), half),
            pltpu.VMEM((groups, ctx_count - 1, 2 * own, 2 * width), half),
            pltpu.VMEM((2 * own, 2 * width), full),
            pltpu.VMEM((groups, 2 * own, model), half),
            pltpu.VMEM((groups, own, model), half),
            pltpu.VMEM((groups, own, model), half),
            pltpu.VMEM((groups, own, model), half),
            dma((groups, ctx_count)),
            dma((groups, ctx_count)),
            dma((groups,)),
            dma((groups,)),
            dma((groups,)),
            dma((groups,)),
            dma,
        ],
        compiler_params=pltpu.CompilerParams(
            collective_id=2, has_side_effects=True, vmem_limit_bytes=60 * 2**20
        ),
    )(pair, query_grad, w_qkv)


def body(state, norm_gain, w_qkv, w_out, probe, noise, segment_ids):
    local_rows, model_width = state.shape
    width = w_qkv.shape[2]
    local_heads = width // HEAD_DIM
    head_count = lax.axis_size("head")
    ctx_count = lax.axis_size("ctx")
    ctx_index = lax.axis_index("ctx")
    own_rows = local_rows // head_count
    row_start = lax.axis_index("head") * own_rows
    w_full = lax.all_gather(w_out, "head", axis=0, tiled=True)
    state_f = state.astype(jnp.float32)
    gain_full = norm_gain.astype(jnp.float32)
    inverse = row_scale(state_f)
    normed = (state_f * inverse * gain_full).astype(jnp.bfloat16)

    def project(index):
        return jnp.dot(normed, w_qkv[index], preferred_element_type=jnp.float32).astype(
            jnp.bfloat16
        )

    query_rows, key_rows, value_rows = project(0), project(1), project(2)
    keys, values, segs = gather_keys(ctx_count, key_rows, value_rows, segment_ids)
    total_rows = keys.shape[0]
    pos = ctx_index * local_rows + jnp.arange(local_rows, dtype=jnp.int32)
    start = jnp.sum((segs[None, :] < segment_ids[:, None]).astype(jnp.int32), axis=1)
    fq, fk = (min(local_rows, size) for size in FORWARD_BLOCKS)
    gq, gk = (min(local_rows, size) for size in BACKWARD_BLOCKS)
    smem = pl.BlockSpec(memory_space=pltpu.SMEM)
    params = pltpu.CompilerParams(vmem_limit_bytes=60 * 2**20)
    outputs, logs = pl.pallas_call(
        functools.partial(forward_kernel, local_heads, fq, fk),
        out_shape=(
            jax.ShapeDtypeStruct((local_rows, width), jnp.bfloat16),
            jax.ShapeDtypeStruct((local_rows // fq, local_heads, fq), jnp.float32),
        ),
        in_specs=[smem] + [VMEM] * 5,
        out_specs=(VMEM, VMEM),
        compiler_params=params,
        cost_estimate=pl.CostEstimate(
            flops=4 * local_rows * total_rows * width, bytes_accessed=0, transcendentals=0
        ),
    )(
        make_table(start, pos, fq, fk),
        query_rows,
        keys,
        values,
        start.reshape(-1, 1, fq),
        pos.reshape(-1, 1, fq),
    )
    state_half = lax.dynamic_slice_in_dim(state, row_start, own_rows, 0)
    probe_own = lax.dynamic_slice_in_dim(probe, row_start, own_rows, 0)
    state_own = state_half.astype(jnp.float32)
    inverse_own = row_scale(state_own)
    grads_out, readout_own = middle(head_count, outputs, w_full, state_half, probe_own)
    query_grad, pair = pl.pallas_call(
        functools.partial(backward_kernel, local_heads, gq, gk),
        out_shape=(
            jax.ShapeDtypeStruct((local_rows, width), jnp.bfloat16),
            jax.ShapeDtypeStruct((total_rows, 2 * width), jnp.bfloat16),
        ),
        in_specs=[smem] + [VMEM] * 8,
        out_specs=(VMEM, VMEM),
        scratch_shapes=[pltpu.VMEM((total_rows, 2 * width), jnp.float32)],
        compiler_params=params,
        cost_estimate=pl.CostEstimate(
            flops=10 * local_rows * total_rows * width, bytes_accessed=0, transcendentals=0
        ),
    )(
        make_table(start, pos, gq, gk),
        query_rows,
        keys,
        values,
        grads_out,
        outputs,
        logs.reshape(local_rows // fq, local_heads, fq),
        start.reshape(-1, 1, gq),
        pos.reshape(-1, 1, gq),
    )
    normed_grad = tail(ctx_count, head_count, pair, query_grad, w_qkv)
    gain_grad = normed_grad * gain_full
    gradient = (
        readout_own
        + inverse_own * gain_grad
        - state_own * inverse_own**3 * jnp.mean(gain_grad * state_own, axis=-1, keepdims=True)
    )
    return state_own - STEP_SIZE * gradient + jnp.sqrt(2.0 * STEP_SIZE) * noise.astype(jnp.float32)


def solution(mesh):
    placed = (
        P("ctx", None),
        P(),
        P(None, None, "head"),
        P("head", None),
        P("ctx", None),
        P(("ctx", "head"), None),
        P("ctx"),
    )
    return jax.shard_map(
        body, mesh=mesh, in_specs=placed, out_specs=P(("ctx", "head"), None), check_vma=False
    )
```

time: 559 us -> 264 us (0.47); the launches traced: 551 us -> 263 us
  Pallas kernels: 0 us -> 225 us
  waiting for transfers between devices: 196 us -> 0.71 us
  matrix products: 198 us -> 9.91 us
  local copies, waits for them, and re-layouts: 68 us -> 2.35 us
  other arithmetic: 64.9 us -> 12.2 us
  blocking collectives: 6.47 us -> 0 us
    pallas_call x0 -> x5, Pallas kernels: none -> 225 us  [the longest x1 101 us: tail(): pl.pallas_call(functools.partial(tail_kernel, ctx_count, number), out_sha...]
    dot_general x34 -> x3, matrix products: 198 us -> 9.91 us  [project(): jnp.dot(normed, w_qkv[index], preferred_element_type=jnp.float32)]
    psum x1 -> x0, waiting for transfers between devices: 95.9 us -> none  [body(): lax.psum(term.astype(jnp.bfloat16), 'head').astype(jnp.float32)]
    all_gather x2 -> x1, waiting for transfers between devices: 57.6 us -> 0.01 us  [body(): w_full = lax.all_gather(w_out, 'head', axis=0, tiled=True)]
    reduce_scatter x2 -> x0, waiting for transfers between devices: 41.7 us -> none  [the longest x1 41.7 us: body(): lax.psum_scatter((running + jnp.einsum('sn,dn->sd', value_grad, w_qkv[2],...]
    dynamic_slice x36 -> x1, local copies, waits for them, and re-layouts: 26.6 us -> 2.31 us  [body(): probe_own = lax.dynamic_slice_in_dim(probe, row_start, own_rows, 0)]
    reduce_sum x5 -> x1, other arithmetic: 20.6 us -> 2.49 us  [body(): jnp.sum((segs[None, :] < segment_ids[:, None]).astype(jnp.int32), axis=1)]
    unnamed x29 -> x14, local copies, waits for them, and re-layouts: 16.1 us -> 0.03 us
  transfers between devices with their start and end apart: 5 -> 1, of which waited for: 4 -> 0; matrix products, arithmetic and copies ran while one was open for 17% -> 8% of each run, Pallas kernels for 0% -> 26%
where the time goes in v1:
time: 264 us; the launch traced here: 263 us
  Pallas kernels  225 us (85%)
  between operations  13.5 us (5%)
  other arithmetic  12.2 us (5%)
  matrix products  9.91 us (4%)
    pallas_call x1, Pallas kernels, tail(): pl.pallas_call(functools.partial(tail_kernel, ctx_count, number), out_sha...  101 us
    pallas_call x1, Pallas kernels, gather_keys(): pl.pallas_call(functools.partial(gather_kernel, number), out_shape=(full,...  49.3 us
    pallas_call x1, Pallas kernels, middle(): pl.pallas_call(functools.partial(middle_kernel, number), out_shape=(jax.S...  36.4 us
    pallas_call x1, Pallas kernels, body(): pl.pallas_call(functools.partial(backward_kernel, local_heads, gq, gk), o...  19 us
    pallas_call x1, Pallas kernels, body(): pl.pallas_call(functools.partial(forward_kernel, local_heads, fq, fk), ou...  18.9 us
    dot_general x3, matrix products, project(): jnp.dot(normed, w_qkv[index], preferred_element_type=jnp.float32)  9.91 us
  transfers between devices with their start and end apart: 1, of which 0 were waited for; matrix products, arithmetic and copies ran while one was open for 8% of the time, Pallas kernels for 26%

profile of v1, /device:TPU:11, one launch (start us, length us, event | category | flops | bytes accessed | tf_op | source)
XLA Modules:
  0.0 263.3 jit_solution(3048322578845008353)
XLA Ops:
  6.5 0.0 all-gather.2.cloned.1.call-start
  6.5 0.7 all-gather.2.cloned.1.call-update
  7.3 0.0 copy-start.1
  7.3 0.8 convert_element_type.29
  8.1 3.3 %fusion = f32[1024]{0:T(1024)S(1)} fusion(bf16[1024,2048]{1,0:T(8,128)(2,1)} %param.7), kind=kLoop, calls=%fused_computation.3 | loop fusion | flops 6290432 | bytes 4198400 | tf_op jit(solution)/shard_map/reduce_sum | solution.py:25
  11.4 0.0 copy-done.1
  11.4 0.0 copy-start.2
  11.4 3.5 %convolution_convert_fusion.1.value_ref = bf16[1024,256]{1,0:T(8,128)(2,1)} fusion(bf16[3,2048,256]{2,1,0:T(8,128)(2,1)} %w_ref.1, bf16[1024,2048]{1,0:T(8,128)(2,1)S(1)} %copy-done.1, f32[2048]{0:T(1024)S(1)} %convert_element_type.29, f32[1024]{0:T(1024)S(1)} %add_rsqrt_fusion), kind=kOutput, calls=%fused_computation.11 | convolution fusion | flops 1082392576 | bytes 5779456 | tf_op jit(solution)/shard_map/dot_general | solution.py:505
  14.9 0.0 copy-done.2
  14.9 0.0 copy-start.5
  14.9 2.1 convolution_convert_fusion.2.key_ref
  17.0 49.3 %shard_map.73 = (bf16[4096,256]{1,0:T(8,128)(2,1)}, bf16[4096,256]{1,0:T(8,128)(2,1)}, s32[4,8,128]{2,1,0:T(8,128)}) custom-call(bf16[1024,256]{1,0:T(8,128)(2,1)} %convolution_convert_fusion.2.key_ref, bf16[1024,256]{1,0:T(8,128)(2,1)} %convolution_convert_fusion.1.value_ref, s32[8,128]{1,0:T(8,128)} %bitcast.12), custom_call_target="tpu_custom_call" | custom-call | tf_op jit(solution)/shard_map/pallas_call | solution.py:78
  66.3 0.0 copy-done.5
  66.3 2.5 convert_reduce_fusion
  68.8 0.0 copy-start.6
  68.9 0.1 fusion.18
  68.9 0.6 pad_add_fusion.table
  69.6 0.6 add_add_fusion.pos_ref
  70.1 2.3 constant_dynamic-slice_fusion
  72.5 4.3 %convolution_convert_fusion.query_ref = bf16[1024,256]{1,0:T(8,128)(2,1)} fusion(bf16[3,2048,256]{2,1,0:T(8,128)(2,1)S(1)} %copy-done.2, bf16[1024,2048]{1,0:T(8,128)(2,1)} %param.7, f32[2048]{0:T(1024)S(1)} %convert_element_type.29, f32[1024]{0:T(1024)S(1)} %add_rsqrt_fusion), kind=kOutput, calls=%fused_computation.10 | convolution fusion | flops 1082392576 | bytes 5779456 | tf_op jit(solution)/shard_map/dot_general | solution.py:505
  76.7 0.0 copy-done.6
  76.7 18.9 %shard_map.74 = (bf16[1024,256]{1,0:T(8,128)(2,1)}, f32[4,2,256]{2,1,0:T(2,128)}) custom-call(s32[4,4]{1,0:T(4,128)} %pad_add_fusion.table, bf16[1024,256]{1,0:T(8,128)(2,1)} %convolution_convert_fusion.query_ref, bf16[4096,256]{1,0:T(8,128)(2,1)} %get-tuple-element.15.key_ref, bf16[4096,256]{1,0:T(8,128)(2,1)} %get-tuple-element.16.value_ref, ...), custom_call_target="tpu_custom_call" | custom-call | flops 4294967296 | tf_op jit(solution)/shard_map/pallas_call | solution.py:518
  95.6 0.0 all-gather.2.cloned.1.call-done.w_any
  95.6 36.4 %shard_map.75 = (bf16[1024,256]{1,0:T(8,128)(2,1)}, f32[128,2048]{1,0:T(8,128)}) custom-call(bf16[1024,256]{1,0:T(8,128)(2,1)} %get-tuple-element.17.part_ref.out_ref, bf16[2048,2048]{1,0:T(8,128)(2,1)} %all-gather.2.cloned.1.call-done.w_any, bf16[128,2048]{1,0:T(8,128)(2,1)} %get-tuple-element.32.state_ref, bf16[128,2048]{1,0:T(8,128)(2,1)} %get-tuple-element.31.probe_ref), custom_call_target="tpu_custom_call" | custom-call | tf_op jit(solution)/shard_map/pallas_call | solution.py:322
  132.1 19.0 %shard_map.76 = (bf16[1024,256]{1,0:T(8,128)(2,1)}, bf16[4096,512]{1,0:T(8,128)(2,1)}) custom-call(s32[4,4]{1,0:T(4,128)} %pad_add_fusion.table, bf16[1024,256]{1,0:T(8,128)(2,1)} %convolution_convert_fusion.query_ref, bf16[4096,256]{1,0:T(8,128)(2,1)} %get-tuple-element.15.key_ref, bf16[4096,256]{1,0:T(8,128)(2,1)} %get-tuple-element.16.value_ref, ...), custom_call_target="tpu_custom_call" | custom-call | flops 10737418240 | tf_op jit(solution)/shard_map/pallas_call | solution.py:543
  151.1 0.0 copy-start
  151.1 0.0 copy-start.3
  151.1 0.0 copy-start.4
  151.1 100.9 %shard_map.77 = f32[128,2048]{1,0:T(8,128)} custom-call(bf16[4096,512]{1,0:T(8,128)(2,1)} %get-tuple-element.21.pair_any, bf16[1024,256]{1,0:T(8,128)(2,1)} %get-tuple-element.22.query_ref, bf16[3,2048,256]{2,1,0:T(8,128)(2,1)} %w_ref.1), custom_call_target="tpu_custom_call" | custom-call | tf_op jit(solution)/shard_map/pallas_call | solution.py:462
  252.0 0.0 copy-done
  252.0 1.5 fusion.3
  253.6 0.0 copy-done.3
  253.6 0.0 copy-done.4
  253.6 2.8 %fusion.8 = f32[128,2048]{1,0:T(8,128)} fusion(bf16[128,2048]{1,0:T(8,128)(2,1)S(1)} %copy-done, bf16[128,2048]{1,0:T(8,128)(2,1)S(1)} %copy-done.4, f32[128,2048]{1,0:T(8,128)S(1)} %copy-done.3, f32[128,2048]{1,0:T(8,128)} %shard_map.77, f32[128]{0:T(128)S(1)} %broadcast_multiply_fusion, f32[128]{0:T(128)S(1)} %get-tuple-element.30, ...), kind=kLoop, calls=%fused_computation.18 | loop fusion | flops 3145728 | bytes 4204032 | tf_op jit(solution)/shard_map/add | solution.py:574
  (5 shorter events, 0.0 us)
Async XLA Ops:
  6.5 89.1 %all-gather.2.cloned.1.call-start = ((), (), s32[]{:S(2)}) async-start(), calls=%async_computation | async-start | bytes 9437184 | tf_op jit(solution)/shard_map/all_gather | solution.py:498
  7.3 4.1 %copy-start.1 = (bf16[1024,2048]{1,0:T(8,128)(2,1)S(1)}, bf16[1024,2048]{1,0:T(8,128)(2,1)}, u32[]{:S(2)}) copy-start(bf16[1024,2048]{1,0:T(8,128)(2,1)} %param.7) | copy-start | bytes 12582916
  11.4 3.5 %copy-start.2 = (bf16[3,2048,256]{2,1,0:T(8,128)(2,1)S(1)}, bf16[3,2048,256]{2,1,0:T(8,128)(2,1)}, u32[]{:S(2)}) copy-start(bf16[3,2048,256]{2,1,0:T(8,128)(2,1)} %w_ref.1) | copy-start | bytes 9437188
  14.9 51.4 %copy-start.5 = (s32[1024]{0:T(1024)S(1)}, s32[1024]{0:T(1024)}, u32[]{:S(2)}) copy-start(s32[1024]{0:T(1024)} %param.13) | copy-start | bytes 12292
  68.8 7.9 %copy-start.6 = (s32[1024]{0:T(1024)}, s32[1024]{0:T(1024)S(1)}, u32[]{:S(2)}) copy-start(s32[1024]{0:T(1024)S(1)} %convert_reduce_fusion) | copy-start | bytes 12292
  151.1 100.9 %copy-start = (bf16[128,2048]{1,0:T(8,128)(2,1)S(1)}, bf16[128,2048]{1,0:T(8,128)(2,1)}, u32[]{:S(2)}) copy-start(bf16[128,2048]{1,0:T(8,128)(2,1)} %get-tuple-element.32.state_ref) | copy-start | bytes 1572868
  151.1 102.5 %copy-start.3 = (f32[128,2048]{1,0:T(8,128)S(1)}, f32[128,2048]{1,0:T(8,128)}, u32[]{:S(2)}) copy-start(f32[128,2048]{1,0:T(8,128)} %get-tuple-element.18) | copy-start | bytes 3145732
  151.1 102.5 %copy-start.4 = (bf16[128,2048]{1,0:T(8,128)(2,1)S(1)}, bf16[128,2048]{1,0:T(8,128)(2,1)}, u32[]{:S(2)}) copy-start(bf16[128,2048]{1,0:T(8,128)(2,1)} %param.12) | copy-start | bytes 1572868
Sparse Core Ops, SparseCore 0:
  8.9 81.1 all-gather.1

commit v2 on v1

--- a/solution.py
+++ b/solution.py
@@ -17,8 +17,8 @@
 ANY = pl.BlockSpec(memory_space=pl.ANY)
 NT = (((1,), (1,)), ((), ()))
 TN = (((0,), (0,)), ((), ()))
-FORWARD_BLOCKS = (256, 512)
-BACKWARD_BLOCKS = (256, 512)
+FORWARD_BLOCKS = (512, 512)
+BACKWARD_BLOCKS = (512, 512)
 
 
 def row_scale(matrix):
@@ -39,55 +39,91 @@
 
 
 def gather_kernel(
-    number, key_ref, value_ref, seg_ref, keys, values, segs, send_sem, recv_sem, own_sem
+    number, key_ref, value_ref, seg_ref, normed_ref, w_ref, keys, values, segs, query_out, send_sem,
+    recv_sem, own_sem,
 ):
     me = lax.axis_index("ctx")
     rows = key_ref.shape[0]
     greet("ctx", number, me)
-    mine = pl.ds(pl.multiple_of(me * rows, rows), rows)
-    pairs = (
-        (key_ref, keys.at[mine]),
-        (value_ref, values.at[mine]),
-        (seg_ref, segs.at[me]),
-    )
+
+    def place(index):
+        return pl.ds(pl.multiple_of(index * rows, rows), rows)
+
+    def send(slot, source, target, peer):
+        copy = pltpu.make_async_remote_copy(
+            src_ref=source,
+            dst_ref=target,
+            send_sem=send_sem.at[slot],
+            recv_sem=recv_sem.at[slot],
+            device_id={"ctx": peer},
+            device_id_type=MESH,
+        )
+        copy.start()
+        return copy
+
+    mine = place(me)
     copies = []
     for step in range(1, number):
-        for index, (source, target) in enumerate(pairs):
-            copy = pltpu.make_async_remote_copy(
-                src_ref=source,
-                dst_ref=target,
-                send_sem=send_sem.at[step, index],
-                recv_sem=recv_sem.at[step, index],
-                device_id={"ctx": lax.rem(me + step, number)},
-                device_id_type=MESH,
-            )
-            copy.start()
-            copies.append(copy)
+        copies.append(send(step, seg_ref, segs.at[me], lax.rem(me + step, number)))
+    relay = number == 4
+    if relay:
+        low, high = lax.rem(me, 2), me // 2
+        across, along = high * 2 + 1 - low, (1 - high) * 2 + low
+        key_first = send(number, key_ref, keys.at[mine], across)
+        value_first = send(number + 1, value_ref, values.at[mine], along)
+        copies.append(send(number + 2, value_ref, values.at[mine], across))
+        copies.append(send(number + 3, key_ref, keys.at[mine], along))
+    else:
+        for step in range(1, number):
+            peer = lax.rem(me + step, number)
+            copies.append(send(number + 2 * step, key_ref, keys.at[mine], peer))
+            copies.append(send(number + 2 * step + 1, value_ref, values.at[mine], peer))
+    pairs = ((key_ref, keys.at[mine]), (value_ref, values.at[mine]), (seg_ref, segs.at[me]))
     for index, (source, target) in enumerate(pairs):
         copy = pltpu.make_async_copy(source, target, own_sem.at[index])
         copy.start()
         copies.append(copy)
+    tile = min(256, rows)
+
+    def project(piece, _):
+        at = pl.ds(pl.multiple_of(piece * tile, tile), tile)
+        query_out[at, :] = jnp.dot(
+            normed_ref[at, :], w_ref[...], preferred_element_type=jnp.float32
+        ).astype(jnp.bfloat16)
+        return 0
+
+    lax.fori_loop(0, rows // tile, project, 0)
+    if relay:
+        key_first.wait()
+        copies.append(send(number + 4, keys.at[place(across)], keys.at[place(across)], along))
+        value_first.wait()
+        copies.append(send(number + 5, values.at[place(along)], values.at[place(along)], across))
     for copy in copies:
         copy.wait()
 
 
-def gather_keys(number, key_rows, value_rows, segment_ids):
+def gather_keys(number, key_rows, value_rows, segment_ids, normed, w_query):
     rows, width = key_rows.shape
     seg = segment_ids.reshape(-1, 128)
     full = jax.ShapeDtypeStruct((number * rows, width), key_rows.dtype)
-    keys, values, segs = pl.pallas_call(
+    keys, values, segs, queries = pl.pallas_call(
         functools.partial(gather_kernel, number),
-        out_shape=(full, full, jax.ShapeDtypeStruct((number,) + seg.shape, seg.dtype)),
-        in_specs=[VMEM] * 3,
-        out_specs=(ANY,) * 3,
+        out_shape=(
+            full,
+            full,
+            jax.ShapeDtypeStruct((number,) + seg.shape, seg.dtype),
+            jax.ShapeDtypeStruct((rows, width), key_rows.dtype),
+        ),
+        in_specs=[VMEM] * 5,
+        out_specs=(ANY, ANY, ANY, VMEM),
         scratch_shapes=[
-            pltpu.SemaphoreType.DMA((number, 3)),
-            pltpu.SemaphoreType.DMA((number, 3)),
+            pltpu.SemaphoreType.DMA((3 * number + 6,)),
+            pltpu.SemaphoreType.DMA((3 * number + 6,)),
             pltpu.SemaphoreType.DMA((3,)),
         ],
         compiler_params=pltpu.CompilerParams(collective_id=0, has_side_effects=True),
-    )(key_rows, value_rows, seg)
-    return keys, values, segs.reshape(-1)
+    )(key_rows, value_rows, seg, normed, w_query)
+    return keys, values, segs.reshape(-1), queries
 
 
 def block_ranges(table, index):
@@ -506,8 +542,10 @@
             jnp.bfloat16
         )
 
-    query_rows, key_rows, value_rows = project(0), project(1), project(2)
-    keys, values, segs = gather_keys(ctx_count, key_rows, value_rows, segment_ids)
+    key_rows, value_rows = project(1), project(2)
+    keys, values, segs, query_rows = gather_keys(
+        ctx_count, key_rows, value_rows, segment_ids, normed, w_qkv[0]
+    )
     total_rows = keys.shape[0]
     pos = ctx_index * local_rows + jnp.arange(local_rows, dtype=jnp.int32)
     start = jnp.sum((segs[None, :] < segment_ids[:, None]).astype(jnp.int32), axis=1)

time: 264 us -> 250 us (0.947)
  Pallas kernels: 225 us -> 202 us
  waiting for transfers between devices: 0.71 us -> 11.3 us
  matrix products: 9.91 us -> 4.17 us
    all_gather x1, waiting for transfers between devices: 0.01 us -> 10.6 us  [body(): w_full = lax.all_gather(w_out, 'head', axis=0, tiled=True)]
    pallas_call x1, Pallas kernels: 101 us -> 92.7 us  [tail(): pl.pallas_call(functools.partial(tail_kernel, ctx_count, number), out_sha...]
    pallas_call x1, Pallas kernels: 49.3 us -> 41.4 us  [gather_keys(): pl.pallas_call(functools.partial(gather_kernel, number), out_shape=(full,...]
    dot_general x3 -> x2, matrix products: 9.91 us -> 4.17 us  [project(): jnp.dot(normed, w_qkv[index], preferred_element_type=jnp.float32)]
    pallas_call x1, Pallas kernels: 18.9 us -> 13.5 us  [body(): pl.pallas_call(functools.partial(forward_kernel, local_heads, fq, fk), ou...]
  transfers between devices with their start and end apart: 1 -> 1, of which waited for: 0 -> 1; matrix products, arithmetic and copies ran while one was open for 8% -> 7% of each run, Pallas kernels for 26% -> 22%
where the time goes in v2:
time: 250 us; the launch traced here: 249 us
  Pallas kernels  202 us (81%)
  between operations  13.5 us (5%)
  other arithmetic  13.3 us (5%)
  waiting for transfers between devices  11.3 us (5%)
  local copies, waits for them, and re-layouts  4.2 us (2%)
  matrix products  4.17 us (2%)
    pallas_call x1, Pallas kernels, tail(): pl.pallas_call(functools.partial(tail_kernel, ctx_count, number), out_sha...  92.7 us
    pallas_call x1, Pallas kernels, gather_keys(): pl.pallas_call(functools.partial(gather_kernel, number), out_shape=(full,...  41.4 us
    pallas_call x1, Pallas kernels, middle(): pl.pallas_call(functools.partial(middle_kernel, number), out_shape=(jax.S...  36.1 us
    pallas_call x1, Pallas kernels, body(): pl.pallas_call(functools.partial(backward_kernel, local_heads, gq, gk), o...  18.6 us
    pallas_call x1, Pallas kernels, body(): pl.pallas_call(functools.partial(forward_kernel, local_heads, fq, fk), ou...  13.5 us
    all_gather x1, waiting for transfers between devices, body(): w_full = lax.all_gather(w_out, 'head', axis=0, tiled=True)  10.6 us
  transfers between devices with their start and end apart: 1, of which 1 were waited for; matrix products, arithmetic and copies ran while one was open for 7% of the time, Pallas kernels for 22%

profile of v2, /device:TPU:11, one launch (start us, length us, event | category | flops | bytes accessed | tf_op | source)
XLA Modules:
  0.0 248.8 jit_solution(6828138583546902247)
XLA Ops:
  6.5 0.0 all-gather.2.cloned.1.call-start
  6.5 0.7 all-gather.2.cloned.1.call-update
  7.3 0.0 copy-start
  7.3 0.8 convert_element_type.26
  8.1 3.3 %fusion = f32[1024]{0:T(1024)S(1)} fusion(bf16[1024,2048]{1,0:T(8,128)(2,1)} %param.7), kind=kLoop, calls=%fused_computation.3 | loop fusion | flops 6290432 | bytes 4198400 | tf_op jit(solution)/shard_map/reduce_sum | solution.py:25
  11.4 0.0 copy-done
  11.4 0.0 copy-start.3
  11.4 1.0 fusion.2.normed_ref
  12.4 0.8 copy-done.3
  13.3 0.0 copy-start.1
  13.3 2.1 convolution_convert_fusion.value_ref
  15.4 2.0 convolution_convert_fusion.1.key_ref
  17.5 0.0 copy-done.1
  17.5 0.0 copy-start.7
  17.5 1.0 slice_bitcast_fusion.w_ref
  18.5 41.4 %shard_map.73 = (bf16[4096,256]{1,0:T(8,128)(2,1)}, bf16[4096,256]{1,0:T(8,128)(2,1)}, s32[4,8,128]{2,1,0:T(8,128)}, bf16[1024,256]{1,0:T(8,128)(2,1)}) custom-call(bf16[1024,256]{1,0:T(8,128)(2,1)} %convolution_convert_fusion.1.key_ref, bf16[1024,256]{1,0:T(8,128)(2,1)} %convolution_convert_fusion.value_ref, s32[8,128]{1,0:T(8,128)} %bitcast.15, ...), custom_call_target="tpu_custom_call" | custom-call | tf_op jit(solution)/shard_map/pallas_call | solution.py:109
  59.9 0.0 copy-done.7
  59.9 2.5 convert_reduce_fusion
  62.4 0.0 copy-start.6
  62.4 0.1 fusion.14
  62.5 0.6 pad_add_fusion.table
  63.1 0.6 add_add_fusion.pos_ref
  63.7 2.3 constant_dynamic-slice_fusion
  66.0 0.0 copy-done.6
  66.0 13.5 %shard_map.74 = (bf16[1024,256]{1,0:T(8,128)(2,1)}, f32[2,2,512]{2,1,0:T(2,128)}) custom-call(s32[2,4]{1,0:T(2,128)} %pad_add_fusion.table, bf16[1024,256]{1,0:T(8,128)(2,1)} %get-tuple-element.16.query_ref, bf16[4096,256]{1,0:T(8,128)(2,1)} %get-tuple-element.17.key_ref, bf16[4096,256]{1,0:T(8,128)(2,1)} %get-tuple-element.18.value_ref, ...), custom_call_target="tpu_custom_call" | custom-call | flops 4294967296 | tf_op jit(solution)/shard_map/pallas_call | solution.py:556
  79.5 10.6 %all-gather.2.cloned.1.call-done.w_any = bf16[2048,2048]{1,0:T(8,128)(2,1)} async-done(((bf16[256,2048]{1,0:T(8,128)(2,1)}), bf16[2048,2048]{1,0:T(8,128)(2,1)}) %all-gather.2.cloned.1.call-update) | async-done | bytes 8388624 | tf_op jit(solution)/shard_map/all_gather | solution.py:534
  90.1 36.1 %shard_map.75 = (bf16[1024,256]{1,0:T(8,128)(2,1)}, f32[128,2048]{1,0:T(8,128)}) custom-call(bf16[1024,256]{1,0:T(8,128)(2,1)} %get-tuple-element.19.part_ref.out_ref, bf16[2048,2048]{1,0:T(8,128)(2,1)} %all-gather.2.cloned.1.call-done.w_any, bf16[128,2048]{1,0:T(8,128)(2,1)} %get-tuple-element.34.state_ref, bf16[128,2048]{1,0:T(8,128)(2,1)} %get-tuple-element.33.probe_ref), custom_call_target="tpu_custom_call" | custom-call | tf_op jit(solution)/shard_map/pallas_call | solution.py:358
  126.2 18.6 %shard_map.76 = (bf16[1024,256]{1,0:T(8,128)(2,1)}, bf16[4096,512]{1,0:T(8,128)(2,1)}) custom-call(s32[2,4]{1,0:T(2,128)} %pad_add_fusion.table, bf16[1024,256]{1,0:T(8,128)(2,1)} %get-tuple-element.16.query_ref, bf16[4096,256]{1,0:T(8,128)(2,1)} %get-tuple-element.17.key_ref, bf16[4096,256]{1,0:T(8,128)(2,1)} %get-tuple-element.18.value_ref, ...), custom_call_target="tpu_custom_call" | custom-call | flops 10737418240 | tf_op jit(solution)/shard_map/pallas_call | solution.py:581
  144.8 0.0 copy-start.2
  144.8 0.0 copy-start.4
  144.8 0.0 copy-start.5
  144.8 92.7 %shard_map.77 = f32[128,2048]{1,0:T(8,128)} custom-call(bf16[4096,512]{1,0:T(8,128)(2,1)} %get-tuple-element.23.pair_any, bf16[1024,256]{1,0:T(8,128)(2,1)} %get-tuple-element.24.query_ref, bf16[3,2048,256]{2,1,0:T(8,128)(2,1)} %w_ref.1), custom_call_target="tpu_custom_call" | custom-call | tf_op jit(solution)/shard_map/pallas_call | solution.py:498
  237.6 0.0 copy-done.2
  237.6 1.5 fusion.3
  239.1 0.0 copy-done.4
  239.1 0.0 copy-done.5
  239.1 2.8 %fusion.8 = f32[128,2048]{1,0:T(8,128)} fusion(bf16[128,2048]{1,0:T(8,128)(2,1)S(1)} %copy-done.2, bf16[128,2048]{1,0:T(8,128)(2,1)S(1)} %copy-done.5, f32[128,2048]{1,0:T(8,128)S(1)} %copy-done.4, f32[128,2048]{1,0:T(8,128)} %shard_map.77, f32[128]{0:T(128)S(1)} %broadcast_multiply_fusion, f32[128]{0:T(128)S(1)} %get-tuple-element.32, ...), kind=kLoop, calls=%fused_computation.17 | loop fusion | flops 3145728 | bytes 4204032 | tf_op jit(solution)/shard_map/add | solution.py:612
  (5 shorter events, 0.0 us)
Async XLA Ops:
  6.5 83.5 %all-gather.2.cloned.1.call-start = ((), (), s32[]{:S(2)}) async-start(), calls=%async_computation | async-start | bytes 9437184 | tf_op jit(solution)/shard_map/all_gather | solution.py:534
  7.3 4.1 %copy-start = (bf16[1024,2048]{1,0:T(8,128)(2,1)S(1)}, bf16[1024,2048]{1,0:T(8,128)(2,1)}, u32[]{:S(2)}) copy-start(bf16[1024,2048]{1,0:T(8,128)(2,1)} %param.7) | copy-start | bytes 12582916
  11.4 1.9 copy-start.3
  13.3 4.2 %copy-start.1 = (bf16[1024,2048]{1,0:T(8,128)(2,1)}, bf16[1024,2048]{1,0:T(8,128)(2,1)S(1)}, u32[]{:S(2)}) copy-start(bf16[1024,2048]{1,0:T(8,128)(2,1)S(1)} %fusion.2.normed_ref) | copy-start | bytes 12582916
  17.5 42.4 %copy-start.7 = (s32[1024]{0:T(1024)S(1)}, s32[1024]{0:T(1024)}, u32[]{:S(2)}) copy-start(s32[1024]{0:T(1024)} %param.13) | copy-start | bytes 12292
  62.4 3.6 %copy-start.6 = (s32[1024]{0:T(1024)}, s32[1024]{0:T(1024)S(1)}, u32[]{:S(2)}) copy-start(s32[1024]{0:T(1024)S(1)} %convert_reduce_fusion) | copy-start | bytes 12292
  144.8 92.8 %copy-start.2 = (bf16[128,2048]{1,0:T(8,128)(2,1)S(1)}, bf16[128,2048]{1,0:T(8,128)(2,1)}, u32[]{:S(2)}) copy-start(bf16[128,2048]{1,0:T(8,128)(2,1)} %get-tuple-element.34.state_ref) | copy-start | bytes 1572868
  144.8 94.3 %copy-start.4 = (f32[128,2048]{1,0:T(8,128)S(1)}, f32[128,2048]{1,0:T(8,128)}, u32[]{:S(2)}) copy-start(f32[128,2048]{1,0:T(8,128)} %get-tuple-element.20) | copy-start | bytes 3145732
  144.8 94.3 %copy-start.5 = (bf16[128,2048]{1,0:T(8,128)(2,1)S(1)}, bf16[128,2048]{1,0:T(8,128)(2,1)}, u32[]{:S(2)}) copy-start(bf16[128,2048]{1,0:T(8,128)(2,1)} %param.12) | copy-start | bytes 1572868
Sparse Core Ops, SparseCore 0:
  8.9 81.1 all-gather.1
